TPU v7x, 32 devices: a whole 2x2x4 slice. The times are simulated.
32 devices in a mesh: rows: 8 (over y, x, core), dim: 4 (over z).
Axes of the slice: x: 2, y: 2, z: 4, core: 2. Of those that a mesh axis runs over, the one named last changes fastest.
Arguments:
- entity_table: float32 [131072, 512], P(('rows', 'dim')), may hold values from -2.5 to 2.5
- relations: float32 [822, 512], replicated, may hold values from -6 to 6
- thresholds: float32 [64], replicated, may hold values from 0.2 to 2
- head_ids: int32 [2048], replicated, may hold values from 0 to 131071
- rel_ids: int32 [2048], replicated, may hold values from 0 to 821
- thr_idx: int32 [2048], replicated, may hold values from 0 to 63
Outputs:
- serving_table: float32 [131072, 512], P('rows', 'dim')
- fraction: float32 [2048], P(('rows', 'dim'))
All inputs are finite; a program needn't handle non-finite values.
Results may differ from a plain program's by a relative error of at most 0.0011.
Values sent between devices are 32-bit elements; how exact they have to be, the bound alone decides.
A program may use at most 128 MiB of HBM per device.

v0:
```python
import functools
import jax
import jax.numpy as jnp
from jax import lax
from jax.sharding import PartitionSpec as P
from jax.experimental import pallas as pl
from jax.experimental.pallas import tpu as pltpu

MESH = pl.DeviceIdType.MESH
sharpness = 2.0
lanes = 128
units = 16


def plan_for(size):
    middles = 2 * bits_of(size) - 1
    entry = 4
    middle = min(2, (units - entry - 1) // middles)
    return (entry,) + (middle,) * middles + (units - entry - middle * middles,)


def bits_of(size):
    assert size & (size - 1) == 0
    return size.bit_length() - 1


def kernel(
    R, N, total_ents, head_ids, rel_ids, thr, thr_idx, rel, table, *others
):
    slabs = others[:-23]
    (
        serving, frac_out,
        tab, low, part, recv, full, qb, lev, frac, fr_rows, fr_dim, fr_sum,
        load_sem, own_sem, a2a_send, a2a_recv, ex_send, ex_recv, f_send, f_recv, g_send, g_recv,
    ) = others[-23:]
    r = lax.axis_index("rows")
    d = lax.axis_index("dim")
    n, width = table.shape
    slab = width // N
    Q = part.shape[0]
    half_q = Q // 2
    chunk = n // units
    plan = plan_for(N)

    load = pltpu.make_async_copy(table, tab, load_sem)
    load.start()

    row_peers = [lax.rem(r + k, R) for k in range(1, R)]
    dim_peers = [lax.rem(d + k, N) for k in range(1, N)]
    barrier = pltpu.get_barrier_semaphore()
    for t in row_peers:
        pl.semaphore_signal(barrier, inc=1, device_id=(t, d), device_id_type=MESH)
    for t in dim_peers:
        pl.semaphore_signal(barrier, inc=1, device_id=(r, t), device_id_type=MESH)
    pl.semaphore_wait(barrier, R + N - 2)

    def slab_rows(source, t, start, rows):
        if slabs:
            return slabs[0].at[t, pl.ds(start, rows), :]
        return source.at[pl.ds(start, rows), pl.ds(pl.multiple_of(t * slab, slab), slab)]

    a2a = []
    starts = [sum(plan[:i]) * chunk for i in range(len(plan))]

    def issue(piece):
        rows = plan[piece] * chunk
        for k, t in enumerate(dim_peers):
            copy = pltpu.make_async_remote_copy(
                src_ref=slab_rows(table, t, starts[piece], rows),
                dst_ref=serving.at[pl.ds(pl.multiple_of(d * n + starts[piece], 8), rows), :],
                send_sem=a2a_send.at[piece, k],
                recv_sem=a2a_recv.at[piece, k],
                device_id=(r, t),
                device_id_type=MESH,
            )
            copy.start()
            a2a.append(copy)

    issue(0)

    load.wait()
    own = pltpu.make_async_copy(
        slab_rows(tab, d, 0, n),
        serving.at[pl.ds(pl.multiple_of(d * n, 8), n), :],
        own_sem,
    )
    own.start()
    first = (r * N + d) * n

    def pick(i, carry):
        base = pl.multiple_of(i * 8, 8)
        rows = []
        for j in range(8):
            local = head_ids[base + j] - first
            owned = jnp.logical_and(local >= 0, local < n)
            row = tab[pl.ds(jnp.clip(local, 0, n - 1), 1), :]
            rows.append(jnp.where(owned, row, jnp.zeros_like(row)))
        part[pl.ds(base, 8), :] = jnp.concatenate(rows, axis=0)
        return carry

    lax.fori_loop(0, Q // 8, pick, 0)

    row_bits = [("rows", b) for b in range(bits_of(R))]
    dim_bits = [("dim", b) for b in range(bits_of(N))]
    orders = [row_bits + dim_bits, row_bits[:1] + row_bits[:0:-1] + dim_bits]
    steps = len(orders[0])
    nrow = len(row_bits)

    def bit_and_peer(axis, b):
        me = r if axis == "rows" else d
        bit = lax.rem(me // (2 ** b), 2)
        other = me + (1 - 2 * bit) * (2 ** b)
        return bit, ((other, d) if axis == "rows" else (r, other))

    def exchange(src, dst, peer, stream, slot):
        copy = pltpu.make_async_remote_copy(
            src_ref=src, dst_ref=dst,
            send_sem=ex_send.at[stream, slot], recv_sem=ex_recv.at[stream, slot],
            device_id=peer, device_id_type=MESH,
        )
        copy.start()
        return copy

    offset = [0, half_q]
    size = half_q
    into = 0
    piece = 1
    for k in range(steps):
        h = size // 2
        copies = []
        for s in range(2):
            bit, peer = bit_and_peer(*orders[s][k])
            gone = pl.multiple_of(offset[s] + (1 - bit) * h, 8)
            copies.append(exchange(
                part.at[pl.ds(gone, h), :],
                recv.at[pl.ds(s * half_q + into, h), :],
                peer, s, k,
            ))
            offset[s] = pl.multiple_of(offset[s] + bit * h, 8)
        if k >= nrow:
            if piece < len(plan) - 1:
                issue(piece)
                piece += 1
        if k == 0:
            def narrow(i, carry):
                at = pl.multiple_of(i * 128, 128)
                low[pl.ds(at, 128), :] = tab[pl.ds(at, 128), :].astype(jnp.bfloat16)
                return carry

            lax.fori_loop(0, n // 128, narrow, 0)
        if k == 1:
            idx = thr_idx[...]

            def choose(t, acc):
                return jnp.where(idx == t, thr[t], acc)

            lev[...] = lax.fori_loop(0, thr.shape[0], choose, jnp.zeros(idx.shape, jnp.float32))
        for s in range(2):
            copies[s].wait()
            if h >= 64:
                def add(i, carry, s=s, into=into):
                    at = pl.ds(pl.multiple_of(offset[s] + i * 64, 8), 64)
                    frm = pl.ds(s * half_q + into + i * 64, 64)
                    part[at, :] = part[at, :] + recv[frm, :]
                    return carry

                lax.fori_loop(0, h // 64, add, 0)
            else:
                at = pl.ds(offset[s], h)
                part[at, :] = part[at, :] + recv[pl.ds(s * half_q + into, h), :]
        into += h
        size = h

    for s in range(2):
        def form(i, carry, s=s):
            base = pl.multiple_of(offset[s] + i * 8, 8)
            rows = [rel[pl.ds(rel_ids[base + j], 1), :] for j in range(8)]
            full[pl.ds(base, 8), :] = part[pl.ds(base, 8), :] * jnp.concatenate(rows, axis=0)
            return carry

        lax.fori_loop(0, size // 8, form, 0)

    def count_pair(q0, q1):
        qb[:lanes, :] = full[pl.ds(q0, lanes), :].astype(jnp.bfloat16)
        qb[lanes:, :] = full[pl.ds(q1, lanes), :].astype(jnp.bfloat16)
        i0 = q0 // lanes
        i1 = q1 // lanes
        level = jnp.concatenate([lev[i0], lev[i1]], axis=1)
        rows = 512

        def tile(i, acc):
            at = pl.multiple_of(i * rows, rows)
            score = lax.dot_general(
                low[pl.ds(at, rows), :], qb[...], (((1,), (1,)), ((), ())),
                preferred_element_type=jnp.float32,
            )
            soft = jax.nn.sigmoid(sharpness * (score - level))
            return acc + jnp.sum(soft.reshape(rows // 8, 8, 2 * lanes), axis=0)

        acc = lax.fori_loop(0, n // rows, tile, jnp.zeros((8, 2 * lanes), jnp.float32))
        share = jnp.sum(acc, axis=0, keepdims=True) * (1.0 / total_ents)
        frac[i0] = share[:, :lanes]
        frac[i1] = share[:, lanes:]

    def count(starts_, rows):
        def body(i, carry):
            count_pair(pl.multiple_of(starts_[0] + i * lanes, lanes), pl.multiple_of(starts_[1] + i * lanes, lanes))
            return carry

        lax.fori_loop(0, rows // lanes, body, 0)

    pending = None
    counted = False
    slot = steps
    for k in reversed(range(steps)):
        copies = []
        there = []
        for s in range(2):
            bit, peer = bit_and_peer(*orders[s][k])
            here = full.at[pl.ds(offset[s], size), :]
            copies.append(exchange(here, here, peer, s, slot))
            there.append(pl.multiple_of(offset[s] + (1 - 2 * bit) * size, 8))
            offset[s] = pl.multiple_of(offset[s] - bit * size, 8)
        slot += 1
        if k >= nrow:
            issue(piece)
            piece += 1
        if pending is not None:
            count(*pending)
            pending = None
        for copy in copies:
            copy.wait()
        size = 2 * size
        if k <= nrow and size >= lanes:
            pending = (there, size // 2) if counted else (list(offset), size)
            counted = True
    count(*pending)

    per = frac.shape[0] // R
    sends = []
    for k, t in enumerate(row_peers):
        copy = pltpu.make_async_remote_copy(
            src_ref=frac.at[pl.ds(t * per, per)],
            dst_ref=fr_rows.at[R - 2 - k],
            send_sem=f_send.at[k], recv_sem=f_recv.at[R - 2 - k],
            device_id=(t, d), device_id_type=MESH,
        )
        copy.start()
        sends.append(copy)
    total = frac[pl.ds(r * per, per)]
    for k in range(R - 1):
        sends[k].wait_send()
        pltpu.make_async_remote_copy(
            src_ref=frac.at[pl.ds(r * per, per)],
            dst_ref=fr_rows.at[k], send_sem=f_send.at[k], recv_sem=f_recv.at[k],
            device_id=(row_peers[k], d), device_id_type=MESH,
        ).wait_recv()
        total = total + fr_rows[k]
    fr_sum[...] = total
    sends = []
    for k, t in enumerate(dim_peers):
        copy = pltpu.make_async_remote_copy(
            src_ref=fr_sum, dst_ref=fr_dim.at[N - 2 - k],
            send_sem=g_send.at[k], recv_sem=g_recv.at[N - 2 - k],
            device_id=(r, t), device_id_type=MESH,
        )
        copy.start()
        sends.append(copy)
    for k in range(N - 1):
        sends[k].wait_send()
        pltpu.make_async_remote_copy(
            src_ref=fr_sum, dst_ref=fr_dim.at[k],
            send_sem=g_send.at[k], recv_sem=g_recv.at[k],
            device_id=(r, dim_peers[k]), device_id_type=MESH,
        ).wait_recv()
        total = total + fr_dim[k]
    frac_out[...] = total
    own.wait()
    for copy in a2a:
        copy.wait()


def shards(entity_table, relations, thresholds, head_ids, rel_ids, thr_idx):
    R = lax.axis_size("rows")
    N = lax.axis_size("dim")
    n, width = entity_table.shape
    Q = head_ids.shape[0]
    blocks = Q // lanes
    per = blocks // R
    steps = bits_of(R) + bits_of(N)
    pieces = len(plan_for(N))
    f32 = jnp.float32
    DMA = pltpu.SemaphoreType.DMA
    smem = pl.BlockSpec(memory_space=pltpu.SMEM)
    vmem = pl.BlockSpec(memory_space=pltpu.VMEM)
    hbm = pl.BlockSpec(memory_space=pl.ANY)
    operands = [head_ids, rel_ids, thresholds, thr_idx.reshape(blocks, 1, lanes), relations, entity_table]
    if (width // N) % lanes:
        operands.append(entity_table.reshape(n, N, width // N).transpose(1, 0, 2))
    serving, share = pl.pallas_call(
        functools.partial(kernel, R, N, n * R * N),
        out_shape=(
            jax.ShapeDtypeStruct((n * N, width // N), f32),
            jax.ShapeDtypeStruct((per, 1, lanes), f32),
        ),
        in_specs=[smem, smem, smem, vmem, vmem] + [hbm] * (len(operands) - 5),
        out_specs=(hbm, vmem),
        scratch_shapes=[
            pltpu.VMEM((n, width), f32),
            pltpu.VMEM((n, width), jnp.bfloat16),
            pltpu.VMEM((Q, width), f32),
            pltpu.VMEM((Q, width), f32),
            pltpu.VMEM((Q, width), f32),
            pltpu.VMEM((2 * lanes, width), jnp.bfloat16),
            pltpu.VMEM((blocks, 1, lanes), f32),
            pltpu.VMEM((blocks, 1, lanes), f32),
            pltpu.VMEM((R - 1, per, 1, lanes), f32),
            pltpu.VMEM((N - 1, per, 1, lanes), f32),
            pltpu.VMEM((per, 1, lanes), f32),
            DMA, DMA,
            DMA((pieces, N - 1)), DMA((pieces, N - 1)),
            DMA((2, 2 * steps)), DMA((2, 2 * steps)),
            DMA((R - 1,)), DMA((R - 1,)),
            DMA((N - 1,)), DMA((N - 1,)),
        ],
        compiler_params=pltpu.CompilerParams(
            collective_id=0, has_side_effects=True, vmem_limit_bytes=60 * 2**20
        ),
    )(*operands)
    mine = Q // (R * N)
    fraction = lax.dynamic_slice(share.reshape(Q // R), (lax.axis_index("dim") * mine,), (mine,))
    return serving, fraction


def solution(mesh):
    placed = (P(("rows", "dim"), None), P(), P(), P(), P(), P())
    return jax.shard_map(
        shards,
        mesh=mesh,
        in_specs=placed,
        out_specs=(P("rows", "dim"), P(("rows", "dim"))),
        check_vma=False,
    )
```

profile of v0, /device:TPU:9, one launch (start us, length us, event | category | flops | bytes accessed | tf_op | source)
XLA Modules:
  0.0 206.9 jit_solution(6439047316747164978)
XLA Ops:
  0.6 199.2 %shard_map.77 = (f32[16384,128]{1,0:T(8,128)}, f32[2,1,128]{2,1,0:T(1,128)}) custom-call(s32[2048]{0:T(1024)} %head_ids.1, s32[2048]{0:T(1024)} %rel_ids.1, f32[64]{0:T(128)} %thr.1, s32[16,1,128]{2,1,0:T(1,128)} %bitcast.2, f32[822,512]{1,0:T(8,128)} %rel.1, f32[4096,512]{1,0:T(8,128)} %table.1), custom_call_target="tpu_custom_call" | custom-call | tf_op jit(solution)/shard_map/pallas_call | solution.py:300
  199.9 1.2 dynamic_slice.3
  201.1 5.9 %copy.9 = f32[16384,128]{1,0:T(8,128)} copy(f32[16384,128]{1,0:T(8,128)} %get-tuple-element.8) | data formatting | bytes 16777216
where the time goes:
time: 210 us; the launch traced here: 207 us
  Pallas kernels  199 us (95%)
  local copies, waits for them, and re-layouts  7.05 us (3%)
    pallas_call x1, Pallas kernels, shards(): pl.pallas_call(functools.partial(kernel, R, N, n * R * N), out_shape=(jax...  199 us
    unnamed x1, local copies, waits for them, and re-layouts  5.85 us

commit v1 on v0

v1 whole, which is shorter than its diff:
```python
import functools
import jax
import jax.numpy as jnp
from jax import lax
from jax.sharding import PartitionSpec as P
from jax.experimental import pallas as pl
from jax.experimental.pallas import tpu as pltpu

MESH = pl.DeviceIdType.MESH
sharpness = 2.0
lanes = 128
units = 16
entry = 4


def bits_of(size):
    assert size & (size - 1) == 0
    return size.bit_length() - 1


def kernel(
    R, N, total_ents, head_ids_, rel_ids_, thr_, thr_idx_, rel_, table, *others
):
    slabs = others[:-38]
    (
        serving, frac_out,
        head_ids, rel_ids, thr, thr_idx, rel, arg_sem,
        tab, low, part, recv, full, zsum, zin, zout, qb, lev, frac, fr_rows, fr_dim, fr_sum, fr_all,
        load_sem, own_sem, a2a_send, a2a_recv, ex_send, ex_recv, z_send, z_recv,
        pair_send, pair_recv, f_send, f_recv, g_send, g_recv, last_sem,
    ) = others[-38:]
    r = lax.axis_index("rows")
    d = lax.axis_index("dim")
    core = lax.rem(r, 2)
    n, width = table.shape
    slab = width // N
    Q = part.shape[0]
    half_q = Q // 2
    nrow = bits_of(R)
    ndim = bits_of(N)

    def slab_rows(t, start, rows):
        if slabs:
            return slabs[0].at[t, pl.ds(start, rows), :]
        return table.at[pl.ds(start, rows), pl.ds(pl.multiple_of(t * slab, slab), slab)]

    load = pltpu.make_async_copy(table, tab, load_sem)
    load.start()
    own = pltpu.make_async_copy(
        slab_rows(d, 0, n),
        serving.at[pl.ds(pl.multiple_of(d * n, 8), n), :],
        own_sem,
    )
    own.start()
    pairs = [(head_ids_, head_ids), (rel_ids_, rel_ids), (thr_, thr), (thr_idx_, thr_idx), (rel_, rel)]
    args = [pltpu.make_async_copy(src, dst, arg_sem.at[i]) for i, (src, dst) in enumerate(pairs)]
    for copy in args:
        copy.start()

    row_peers = [lax.rem(r + k, R) for k in range(1, R)]
    dim_peers = [lax.rem(d + k, N) for k in range(1, N)]
    barrier = pltpu.get_barrier_semaphore()
    for t in row_peers:
        pl.semaphore_signal(barrier, inc=1, device_id=(t, d), device_id_type=MESH)
    for t in dim_peers:
        pl.semaphore_signal(barrier, inc=1, device_id=(r, t), device_id_type=MESH)
    pl.semaphore_wait(barrier, R + N - 2)

    first_rows = n * entry // units

    def slab_copies(piece):
        start, rows = ((0, first_rows), (first_rows, n - first_rows))[piece]
        return [
            pltpu.make_async_remote_copy(
                src_ref=slab_rows(t, start, rows),
                dst_ref=serving.at[pl.ds(pl.multiple_of(d * n + start, 8), rows), :],
                send_sem=a2a_send.at[piece, k],
                recv_sem=a2a_recv.at[piece, k],
                device_id=(r, t),
                device_id_type=MESH,
            )
            for k, t in enumerate(dim_peers)
        ]

    a2a = [slab_copies(0), slab_copies(1)]
    for copy in a2a[0]:
        copy.start()

    @pl.when(core == 0)
    def _():
        for copy in a2a[1]:
            copy.start()

    for copy in args:
        copy.wait()
    load.wait()
    first = (r * N + d) * n

    def pick(i, carry):
        base = pl.multiple_of(i * 8, 8)
        rows = []
        for j in range(8):
            local = head_ids[base + j] - first
            owned = jnp.logical_and(local >= 0, local < n)
            row = tab[pl.ds(jnp.clip(local, 0, n - 1), 1), :]
            rows.append(jnp.where(owned, row, jnp.zeros_like(row)))
        part[pl.ds(base, 8), :] = jnp.concatenate(rows, axis=0)
        return carry

    lax.fori_loop(0, Q // 8, pick, 0)

    def bit_and_other(me, b):
        bit = lax.rem(me // (2 ** b), 2)
        return bit, me + (1 - 2 * bit) * (2 ** b)

    def remote(src, dst, sems, at, peer):
        return pltpu.make_async_remote_copy(
            src_ref=src, dst_ref=dst, send_sem=sems[0].at[at], recv_sem=sems[1].at[at],
            device_id=peer, device_id_type=MESH,
        )

    def add_rows(h, dst, dst_at, src, src_at, extra, extra_at):
        rows = min(64, h)

        def add(i, carry):
            step = i * rows
            dst[pl.ds(pl.multiple_of(dst_at + step, 8), rows), :] = (
                src[pl.ds(pl.multiple_of(src_at + step, 8), rows), :]
                + extra[pl.ds(pl.multiple_of(extra_at + step, 8), rows), :]
            )
            return carry

        lax.fori_loop(0, h // rows, add, 0)

    row_bits = list(range(nrow))
    orders = [row_bits, row_bits[:1] + row_bits[:0:-1]]
    ex = (ex_send, ex_recv)

    offset = [0, half_q]
    size = half_q
    into = 0
    for k in range(nrow):
        h = size // 2
        copies = []
        for s in range(2):
            bit, other = bit_and_other(r, orders[s][k])
            gone = pl.multiple_of(offset[s] + (1 - bit) * h, 8)
            copy = remote(
                part.at[pl.ds(gone, h), :],
                recv.at[pl.ds(s * half_q + into, h), :],
                ex, (s, k), (other, d),
            )
            copy.start()
            copies.append(copy)
            offset[s] = pl.multiple_of(offset[s] + bit * h, 8)
        if k == 0:
            def narrow(i, carry):
                at = pl.multiple_of(i * 128, 128)
                low[pl.ds(at, 128), :] = tab[pl.ds(at, 128), :].astype(jnp.bfloat16)
                return carry

            lax.fori_loop(0, n // 128, narrow, 0)
        if k == 1:
            idx = thr_idx[...]

            def choose(t, acc):
                return jnp.where(idx == t, thr[t], acc)

            lev[...] = lax.fori_loop(0, thr.shape[0], choose, jnp.zeros(idx.shape, jnp.float32))
        for s in range(2):
            copies[s].wait()
            if k < nrow - 1:
                add_rows(h, part, offset[s], part, offset[s], recv, s * half_q + into)
            else:
                add_rows(h, zsum, (2 * s + core) * h, part, offset[s], recv, s * half_q + into)
        into += h
        size = h

    partner = (r + 1 - 2 * core, d)
    skip = half_q // 2
    core0_at = [pl.multiple_of(offset[s] - core * skip, 8) for s in range(2)]
    pair = (pair_send, pair_recv)
    there_ = [
        remote(zsum.at[pl.ds(2 * s * size, size), :], zsum.at[pl.ds(2 * s * size, size), :], pair, (0, s), partner)
        for s in range(2)
    ]
    back = [
        remote(zout.at[pl.ds(2 * s * size, size), :], full.at[pl.ds(core0_at[s], size), :], pair, (1, s), partner)
        for s in range(2)
    ]
    zx = (z_send, z_recv)

    @pl.when(core == 0)
    def _():
        for copy in there_:
            copy.start()
        for copy in there_:
            copy.wait_send()
        for copy in back:
            copy.wait_recv()

    @pl.when(core == 1)
    def _():
        for copy in there_:
            copy.wait_recv()
        at, count_, into = 0, 4 * size, 0
        for b in range(ndim):
            h = count_ // 2
            bit, other = bit_and_other(d, b)
            gone = pl.multiple_of(at + (1 - bit) * h, 8)
            copy = remote(zsum.at[pl.ds(gone, h), :], zin.at[pl.ds(into, h), :], zx, b, (r, other))
            copy.start()
            at = pl.multiple_of(at + bit * h, 8)
            copy.wait()
            add_rows(h, zsum, at, zsum, at, zin, into)
            into += h
            count_ = h

        def form(i, carry):
            z = pl.multiple_of(at + i * 8, 8)
            slot = z // size
            s = slot // 2
            c = slot - 2 * s
            q = (1 - s) * core0_at[0] + s * core0_at[1] + c * skip + (z - slot * size)
            rows = [rel[pl.ds(rel_ids[q + j], 1), :] for j in range(8)]
            zout[pl.ds(z, 8), :] = zsum[pl.ds(z, 8), :] * jnp.concatenate(rows, axis=0)
            return carry

        lax.fori_loop(0, count_ // 8, form, 0)
        for b in reversed(range(ndim)):
            bit, other = bit_and_other(d, b)
            here = zout.at[pl.ds(at, count_), :]
            copy = remote(here, here, zx, ndim + b, (r, other))
            copy.start()
            if b == 0:
                for late in a2a[1]:
                    late.start()
            copy.wait()
            at = pl.multiple_of(at - bit * count_, 8)
            count_ = 2 * count_
        for copy in back:
            copy.start()
        for s in range(2):
            rows = min(64, size)

            def take(i, carry, s=s):
                step = i * rows
                full[pl.ds(pl.multiple_of(offset[s] + step, 8), rows), :] = (
                    zout[pl.ds(pl.multiple_of((2 * s + 1) * size + step, 8), rows), :]
                )
                return carry

            lax.fori_loop(0, size // rows, take, 0)
        for copy in back:
            copy.wait_send()

    def count_pair(q0, q1):
        qb[:lanes, :] = full[pl.ds(q0, lanes), :].astype(jnp.bfloat16)
        qb[lanes:, :] = full[pl.ds(q1, lanes), :].astype(jnp.bfloat16)
        i0 = q0 // lanes
        i1 = q1 // lanes
        level = jnp.concatenate([lev[i0], lev[i1]], axis=1)
        rows = 512

        def tile(i, acc):
            at = pl.multiple_of(i * rows, rows)
            score = lax.dot_general(
                low[pl.ds(at, rows), :], qb[...], (((1,), (1,)), ((), ())),
                preferred_element_type=jnp.float32,
            )
            soft = jax.nn.sigmoid(sharpness * (score - level))
            return acc + jnp.sum(soft.reshape(rows // 8, 8, 2 * lanes), axis=0)

        acc = lax.fori_loop(0, n // rows, tile, jnp.zeros((8, 2 * lanes), jnp.float32))
        share = jnp.sum(acc, axis=0, keepdims=True) * (1.0 / total_ents)
        frac[i0] = share[:, :lanes]
        frac[i1] = share[:, lanes:]

    def count(starts_, rows):
        def body(i, carry):
            count_pair(pl.multiple_of(starts_[0] + i * lanes, lanes), pl.multiple_of(starts_[1] + i * lanes, lanes))
            return carry

        lax.fori_loop(0, rows // lanes, body, 0)

    pending = None
    counted = False
    if size >= lanes:
        pending = (list(offset), size)
        counted = True
    for k in reversed(range(nrow)):
        copies = []
        there = []
        for s in range(2):
            bit, other = bit_and_other(r, orders[s][k])
            here = full.at[pl.ds(offset[s], size), :]
            copy = remote(here, here, ex, (s, nrow + k), (other, d))
            copy.start()
            copies.append(copy)
            there.append(pl.multiple_of(offset[s] + (1 - 2 * bit) * size, 8))
            offset[s] = pl.multiple_of(offset[s] - bit * size, 8)
        if pending is not None:
            count(*pending)
            pending = None
        for copy in copies:
            copy.wait()
        size = 2 * size
        if size >= lanes:
            pending = (there, size // 2) if counted else (list(offset), size)
            counted = True
    count(*pending)

    per = frac.shape[0] // R
    chips = R // 2

    def row_share(k):
        t = 2 * lax.rem(r // 2 + k, chips)
        slot = R - 2 * k - 1 + core if k else 0
        return pltpu.make_async_remote_copy(
            src_ref=frac.at[pl.ds(t * per, 2 * per)], dst_ref=fr_rows.at[slot],
            send_sem=f_send.at[k], recv_sem=f_recv.at[slot],
            device_id=(t, d), device_id_type=MESH,
        )

    shares = [row_share(k) for k in range(chips)]
    last = pltpu.make_async_remote_copy(
        src_ref=fr_all, dst_ref=fr_all, send_sem=last_sem.at[0], recv_sem=last_sem.at[1],
        device_id=partner, device_id_type=MESH,
    )
    for copy in shares[1:]:
        copy.start()

    @pl.when(core == 1)
    def _():
        shares[0].start()
        shares[0].wait_send()

    for copy in shares[1:]:
        copy.wait_send()

    @pl.when(core == 0)
    def _():
        total = frac[pl.ds(r * per, 2 * per)]
        for k in range(R - 1):
            pltpu.make_async_remote_copy(
                src_ref=frac.at[pl.ds(r * per, 2 * per)], dst_ref=fr_rows.at[k],
                send_sem=f_send.at[0], recv_sem=f_recv.at[k],
                device_id=(row_peers[k], d), device_id_type=MESH,
            ).wait_recv()
            total = total + fr_rows[k]
        fr_sum[...] = total
        sends = []
        for k, t in enumerate(dim_peers):
            copy = pltpu.make_async_remote_copy(
                src_ref=fr_sum, dst_ref=fr_dim.at[N - 2 - k],
                send_sem=g_send.at[k], recv_sem=g_recv.at[N - 2 - k],
                device_id=(r, t), device_id_type=MESH,
            )
            copy.start()
            sends.append(copy)
        for k in range(N - 1):
            sends[k].wait_send()
            pltpu.make_async_remote_copy(
                src_ref=fr_sum, dst_ref=fr_dim.at[k],
                send_sem=g_send.at[k], recv_sem=g_recv.at[k],
                device_id=(r, dim_peers[k]), device_id_type=MESH,
            ).wait_recv()
            total = total + fr_dim[k]
        fr_all[...] = total
        last.start()
        last.wait_send()

    @pl.when(core == 1)
    def _():
        last.wait_recv()

    mine = frac_out.shape[1]
    row = fr_all[core * per + d * mine // lanes]
    place = lax.rem(d * mine, lanes) // mine
    out = row[:, :mine]
    for j in range(1, lanes // mine):
        out = jnp.where(place == j, row[:, j * mine:(j + 1) * mine], out)
    frac_out[...] = out
    own.wait()
    for copies in a2a:
        for copy in copies:
            copy.wait()


def shards(entity_table, relations, thresholds, head_ids, rel_ids, thr_idx):
    R = lax.axis_size("rows")
    N = lax.axis_size("dim")
    n, width = entity_table.shape
    Q = head_ids.shape[0]
    blocks = Q // lanes
    per = blocks // R
    group = 2 * Q // R
    f32 = jnp.float32
    DMA = pltpu.SemaphoreType.DMA
    vmem = pl.BlockSpec(memory_space=pltpu.VMEM)
    hbm = pl.BlockSpec(memory_space=pltpu.HBM)
    anywhere = pl.BlockSpec(memory_space=pl.ANY)
    mine = Q // (R * N)
    operands = [head_ids, rel_ids, thresholds, thr_idx.reshape(blocks, 1, lanes), relations, entity_table]
    if (width // N) % lanes:
        operands.append(entity_table.reshape(n, N, width // N).transpose(1, 0, 2))
    serving, share = pl.pallas_call(
        functools.partial(kernel, R, N, n * R * N),
        out_shape=(
            pltpu.VMEM((n * N, width // N), f32),
            jax.ShapeDtypeStruct((1, mine), f32),
        ),
        in_specs=[hbm] * len(operands),
        out_specs=(anywhere, vmem),
        scratch_shapes=[
            pltpu.SMEM((Q,), jnp.int32),
            pltpu.SMEM((Q,), jnp.int32),
            pltpu.SMEM(thresholds.shape, f32),
            pltpu.VMEM((blocks, 1, lanes), jnp.int32),
            pltpu.VMEM(relations.shape, f32),
            DMA((5,)),
            pltpu.VMEM((n, width), f32),
            pltpu.VMEM((n, width), jnp.bfloat16),
            pltpu.VMEM((Q, width), f32),
            pltpu.VMEM((Q, width), f32),
            pltpu.VMEM((Q, width), f32),
            pltpu.VMEM((group, width), f32),
            pltpu.VMEM((group, width), f32),
            pltpu.VMEM((group, width), f32),
            pltpu.VMEM((2 * lanes, width), jnp.bfloat16),
            pltpu.VMEM((blocks, 1, lanes), f32),
            pltpu.VMEM((blocks, 1, lanes), f32),
            pltpu.VMEM((R - 1, 2 * per, 1, lanes), f32),
            pltpu.VMEM((N - 1, 2 * per, 1, lanes), f32),
            pltpu.VMEM((2 * per, 1, lanes), f32),
            pltpu.VMEM((2 * per, 1, lanes), f32),
            DMA, DMA,
            DMA((2, N - 1)), DMA((2, N - 1)),
            DMA((2, 2 * bits_of(R))), DMA((2, 2 * bits_of(R))),
            DMA((2 * bits_of(N),)), DMA((2 * bits_of(N),)),
            DMA((2, 2)), DMA((2, 2)),
            DMA((R // 2,)), DMA((R - 1,)),
            DMA((N - 1,)), DMA((N - 1,)),
            DMA((2,)),
        ],
        compiler_params=pltpu.CompilerParams(
            collective_id=0, has_side_effects=True, vmem_limit_bytes=40 * 2**20
        ),
    )(*[pltpu.with_memory_space_constraint(x, pltpu.HBM) for x in operands])
    return serving, share.reshape(mine)


def solution(mesh):
    placed = (P(("rows", "dim"), None), P(), P(), P(), P(), P())
    return jax.shard_map(
        shards,
        mesh=mesh,
        in_specs=placed,
        out_specs=(P("rows", "dim"), P(("rows", "dim"))),
        check_vma=False,
    )
```

time: 210 us -> 202 us (0.962); the launches traced: 207 us -> 202 us
  local copies, waits for them, and re-layouts: 7.05 us -> 3.91 us
    unnamed x1 -> x2, local copies, waits for them, and re-layouts: 5.85 us -> 3.91 us
where the time goes in v1:
time: 202 us
  Pallas kernels  197 us (98%)
  local copies, waits for them, and re-layouts  3.91 us (2%)
    pallas_call x1, Pallas kernels, shards(): pl.pallas_call(functools.partial(kernel, R, N, n * R * N), out_shape=(plt...  197 us

profile of v1, /device:TPU:9, one launch (start us, length us, event | category | flops | bytes accessed | tf_op | source)
XLA Modules:
  0.0 201.7 jit_solution(8253321412719698123)
XLA Ops:
  0.6 197.2 %shard_map.77 = (f32[16384,128]{1,0:T(8,128)S(1)}, f32[1,64]{1,0:T(1,128)S(1)}) custom-call(s32[2048]{0:T(1024)} %head_ids_.1, s32[2048]{0:T(1024)} %rel_ids_.1, f32[64]{0:T(128)} %thr_.1, s32[16,1,128]{2,1,0:T(1,128)} %bitcast.3, f32[822,512]{1,0:T(8,128)} %rel_.1, f32[4096,512]{1,0:T(8,128)} %table.1), custom_call_target="tpu_custom_call" | custom-call | tf_op jit(solution)/shard_map/pallas_call | solution.py:407
  197.8 3.4 %copy.10 = f32[16384,128]{1,0:T(8,128)} copy(f32[16384,128]{1,0:T(8,128)S(1)} %get-tuple-element.6) | data formatting | bytes 16777216
  201.2 0.5 copy.11

commit v2 on v1

--- a/solution.py
+++ b/solution.py
@@ -21,14 +21,14 @@
 def kernel(
     R, N, total_ents, head_ids_, rel_ids_, thr_, thr_idx_, rel_, table, *others
 ):
-    slabs = others[:-38]
+    slabs = others[:-40]
     (
         serving, frac_out,
         head_ids, rel_ids, thr, thr_idx, rel, arg_sem,
-        tab, low, part, recv, full, zsum, zin, zout, qb, lev, frac, fr_rows, fr_dim, fr_sum, fr_all,
+        tab, low, part, recv, full, zsum, zin, zout, qb, lev, frac, fr_pair, fr_in, fr_dim, fr_sum, fr_all,
         load_sem, own_sem, a2a_send, a2a_recv, ex_send, ex_recv, z_send, z_recv,
-        pair_send, pair_recv, f_send, f_recv, g_send, g_recv, last_sem,
-    ) = others[-38:]
+        pair_send, pair_recv, f_send, f_recv, g_send, g_recv, last_send, last_recv,
+    ) = others[-40:]
     r = lax.axis_index("rows")
     d = lax.axis_index("dim")
     core = lax.rem(r, 2)
@@ -44,6 +44,23 @@
             return slabs[0].at[t, pl.ds(start, rows), :]
         return table.at[pl.ds(start, rows), pl.ds(pl.multiple_of(t * slab, slab), slab)]
 
+    def bit_and_other(me, b):
+        bit = lax.rem(me // (2 ** b), 2)
+        return bit, me + (1 - 2 * bit) * (2 ** b)
+
+    row_peers = [bit_and_other(r, b)[1] for b in range(nrow)]
+    dim_peers = []
+    for k in range(1, N):
+        t = d
+        for b in range(ndim):
+            if k // 2 ** b % 2:
+                t = t + (bit_and_other(d, b)[1] - d)
+        dim_peers.append(t)
+    barrier = pltpu.get_barrier_semaphore()
+    for t in dim_peers:
+        pl.semaphore_signal(barrier, inc=1, device_id=(r, t), device_id_type=MESH)
+    for t in row_peers:
+        pl.semaphore_signal(barrier, inc=1, device_id=(t, d), device_id_type=MESH)
     load = pltpu.make_async_copy(table, tab, load_sem)
     load.start()
     own = pltpu.make_async_copy(
@@ -56,15 +73,7 @@
     args = [pltpu.make_async_copy(src, dst, arg_sem.at[i]) for i, (src, dst) in enumerate(pairs)]
     for copy in args:
         copy.start()
-
-    row_peers = [lax.rem(r + k, R) for k in range(1, R)]
-    dim_peers = [lax.rem(d + k, N) for k in range(1, N)]
-    barrier = pltpu.get_barrier_semaphore()
-    for t in row_peers:
-        pl.semaphore_signal(barrier, inc=1, device_id=(t, d), device_id_type=MESH)
-    for t in dim_peers:
-        pl.semaphore_signal(barrier, inc=1, device_id=(r, t), device_id_type=MESH)
-    pl.semaphore_wait(barrier, R + N - 2)
+    pl.semaphore_wait(barrier, len(row_peers) + len(dim_peers))
 
     first_rows = n * entry // units
 
@@ -108,10 +117,6 @@
         return carry
 
     lax.fori_loop(0, Q // 8, pick, 0)
-
-    def bit_and_other(me, b):
-        bit = lax.rem(me // (2 ** b), 2)
-        return bit, me + (1 - 2 * bit) * (2 ** b)
 
     def remote(src, dst, sems, at, peer):
         return pltpu.make_async_remote_copy(
@@ -311,68 +316,48 @@
     count(*pending)
 
     per = frac.shape[0] // R
-    chips = R // 2
-
-    def row_share(k):
-        t = 2 * lax.rem(r // 2 + k, chips)
-        slot = R - 2 * k - 1 + core if k else 0
-        return pltpu.make_async_remote_copy(
-            src_ref=frac.at[pl.ds(t * per, 2 * per)], dst_ref=fr_rows.at[slot],
-            send_sem=f_send.at[k], recv_sem=f_recv.at[slot],
-            device_id=(t, d), device_id_type=MESH,
-        )
-
-    shares = [row_share(k) for k in range(chips)]
-    last = pltpu.make_async_remote_copy(
-        src_ref=fr_all, dst_ref=fr_all, send_sem=last_sem.at[0], recv_sem=last_sem.at[1],
-        device_id=partner, device_id_type=MESH,
-    )
-    for copy in shares[1:]:
-        copy.start()
+    fx = (f_send, f_recv)
+    handed = remote(frac, fr_pair, fx, 0, partner)
+    last = remote(fr_all, fr_all, (last_send, last_recv), 0, partner)
 
     @pl.when(core == 1)
     def _():
-        shares[0].start()
-        shares[0].wait_send()
-
-    for copy in shares[1:]:
-        copy.wait_send()
+        handed.start()
+        handed.wait_send()
+        last.wait_recv()
 
     @pl.when(core == 0)
     def _():
-        total = frac[pl.ds(r * per, 2 * per)]
-        for k in range(R - 1):
-            pltpu.make_async_remote_copy(
-                src_ref=frac.at[pl.ds(r * per, 2 * per)], dst_ref=fr_rows.at[k],
-                send_sem=f_send.at[0], recv_sem=f_recv.at[k],
-                device_id=(row_peers[k], d), device_id_type=MESH,
-            ).wait_recv()
-            total = total + fr_rows[k]
+        handed.wait_recv()
+        frac[...] = frac[...] + fr_pair[...]
+        at, held, into = 0, frac.shape[0], 0
+        for b in reversed(range(1, nrow)):
+            h = held // 2
+            bit, other = bit_and_other(r, b)
+            copy = remote(frac.at[pl.ds(at + (1 - bit) * h, h)], fr_in.at[pl.ds(into, h)], fx, b, (other, d))
+            copy.start()
+            at = at + bit * h
+            copy.wait()
+            frac[pl.ds(at, h)] = frac[pl.ds(at, h)] + fr_in[pl.ds(into, h)]
+            into += h
+            held = h
+        total = frac[pl.ds(at, held)]
         fr_sum[...] = total
         sends = []
         for k, t in enumerate(dim_peers):
             copy = pltpu.make_async_remote_copy(
-                src_ref=fr_sum, dst_ref=fr_dim.at[N - 2 - k],
-                send_sem=g_send.at[k], recv_sem=g_recv.at[N - 2 - k],
+                src_ref=fr_sum, dst_ref=fr_dim.at[k],
+                send_sem=g_send.at[k], recv_sem=g_recv.at[k],
                 device_id=(r, t), device_id_type=MESH,
             )
             copy.start()
             sends.append(copy)
         for k in range(N - 1):
-            sends[k].wait_send()
-            pltpu.make_async_remote_copy(
-                src_ref=fr_sum, dst_ref=fr_dim.at[k],
-                send_sem=g_send.at[k], recv_sem=g_recv.at[k],
-                device_id=(r, dim_peers[k]), device_id_type=MESH,
-            ).wait_recv()
+            sends[k].wait()
             total = total + fr_dim[k]
         fr_all[...] = total
         last.start()
         last.wait_send()
-
-    @pl.when(core == 1)
-    def _():
-        last.wait_recv()
 
     mine = frac_out.shape[1]
     row = fr_all[core * per + d * mine // lanes]
@@ -430,7 +415,8 @@
             pltpu.VMEM((2 * lanes, width), jnp.bfloat16),
             pltpu.VMEM((blocks, 1, lanes), f32),
             pltpu.VMEM((blocks, 1, lanes), f32),
-            pltpu.VMEM((R - 1, 2 * per, 1, lanes), f32),
+            pltpu.VMEM((blocks, 1, lanes), f32),
+            pltpu.VMEM((blocks, 1, lanes), f32),
             pltpu.VMEM((N - 1, 2 * per, 1, lanes), f32),
             pltpu.VMEM((2 * per, 1, lanes), f32),
             pltpu.VMEM((2 * per, 1, lanes), f32),
@@ -439,9 +425,9 @@
             DMA((2, 2 * bits_of(R))), DMA((2, 2 * bits_of(R))),
             DMA((2 * bits_of(N),)), DMA((2 * bits_of(N),)),
             DMA((2, 2)), DMA((2, 2)),
-            DMA((R // 2,)), DMA((R - 1,)),
+            DMA((bits_of(R),)), DMA((bits_of(R),)),
             DMA((N - 1,)), DMA((N - 1,)),
-            DMA((2,)),
+            DMA((1,)), DMA((1,)),
         ],
         compiler_params=pltpu.CompilerParams(
             collective_id=0, has_side_effects=True, vmem_limit_bytes=40 * 2**20

time: 202 us -> 200 us (0.990)
  no operation moved by 1% of the time
where the time goes in v2:
time: 200 us
  Pallas kernels  196 us (98%)
  local copies, waits for them, and re-layouts  3.91 us (2%)
    pallas_call x1, Pallas kernels, shards(): pl.pallas_call(functools.partial(kernel, R, N, n * R * N), out_shape=(plt...  196 us

profile of v2, /device:TPU:9, one launch (start us, length us, event | category | flops | bytes accessed | tf_op | source)
XLA Modules:
  0.0 200.2 jit_solution(15466532712184117064)
XLA Ops:
  0.6 195.7 %shard_map.77 = (f32[16384,128]{1,0:T(8,128)S(1)}, f32[1,64]{1,0:T(1,128)S(1)}) custom-call(s32[2048]{0:T(1024)} %head_ids_.1, s32[2048]{0:T(1024)} %rel_ids_.1, f32[64]{0:T(128)} %thr_.1, s32[16,1,128]{2,1,0:T(1,128)} %bitcast.3, f32[822,512]{1,0:T(8,128)} %rel_.1, f32[4096,512]{1,0:T(8,128)} %table.1), custom_call_target="tpu_custom_call" | custom-call | tf_op jit(solution)/shard_map/pallas_call | solution.py:392
  196.3 3.4 %copy.10 = f32[16384,128]{1,0:T(8,128)} copy(f32[16384,128]{1,0:T(8,128)S(1)} %get-tuple-element.6) | data formatting | bytes 16777216
  199.7 0.5 copy.11

commit v3 on v2

--- a/solution.py
+++ b/solution.py
@@ -10,7 +10,7 @@
 sharpness = 2.0
 lanes = 128
 units = 16
-entry = 4
+entry = 3
 
 
 def bits_of(size):
@@ -21,14 +21,14 @@
 def kernel(
     R, N, total_ents, head_ids_, rel_ids_, thr_, thr_idx_, rel_, table, *others
 ):
-    slabs = others[:-40]
+    slabs = others[:-41]
     (
         serving, frac_out,
         head_ids, rel_ids, thr, thr_idx, rel, arg_sem,
         tab, low, part, recv, full, zsum, zin, zout, qb, lev, frac, fr_pair, fr_in, fr_dim, fr_sum, fr_all,
         load_sem, own_sem, a2a_send, a2a_recv, ex_send, ex_recv, z_send, z_recv,
-        pair_send, pair_recv, f_send, f_recv, g_send, g_recv, last_send, last_recv,
-    ) = others[-40:]
+        pair_send, pair_recv, f_send, f_recv, g_send, g_recv, last_send, last_recv, answer,
+    ) = others[-41:]
     r = lax.axis_index("rows")
     d = lax.axis_index("dim")
     core = lax.rem(r, 2)
@@ -48,7 +48,6 @@
         bit = lax.rem(me // (2 ** b), 2)
         return bit, me + (1 - 2 * bit) * (2 ** b)
 
-    row_peers = [bit_and_other(r, b)[1] for b in range(nrow)]
     dim_peers = []
     for k in range(1, N):
         t = d
@@ -56,11 +55,29 @@
             if k // 2 ** b % 2:
                 t = t + (bit_and_other(d, b)[1] - d)
         dim_peers.append(t)
+    def ahead(j):
+        return (r, lax.rem(d + j, N)), d + j < N
+
+    def behind(j):
+        return (r, lax.rem(d + N - j, N)), d >= j
+
+    row_pairs = [bit_and_other(r, b) for b in range(nrow)]
     barrier = pltpu.get_barrier_semaphore()
-    for t in dim_peers:
-        pl.semaphore_signal(barrier, inc=1, device_id=(r, t), device_id_type=MESH)
-    for t in row_peers:
-        pl.semaphore_signal(barrier, inc=1, device_id=(t, d), device_id_type=MESH)
+    leaders = d
+    for j in range(1, N):
+        peer, leads = ahead(j)
+
+        @pl.when(leads)
+        def _(peer=peer):
+            pl.semaphore_signal(barrier, inc=1, device_id=peer, device_id_type=MESH)
+
+    for bit, other in row_pairs:
+        leaders = leaders + bit
+
+        @pl.when(bit == 0)
+        def _(other=other):
+            pl.semaphore_signal(barrier, inc=1, device_id=(other, d), device_id_type=MESH)
+
     load = pltpu.make_async_copy(table, tab, load_sem)
     load.start()
     own = pltpu.make_async_copy(
@@ -73,7 +90,22 @@
     args = [pltpu.make_async_copy(src, dst, arg_sem.at[i]) for i, (src, dst) in enumerate(pairs)]
     for copy in args:
         copy.start()
-    pl.semaphore_wait(barrier, len(row_peers) + len(dim_peers))
+
+    @pl.when(leaders > 0)
+    def _():
+        pl.semaphore_wait(barrier, leaders)
+
+    for j in range(1, N):
+        peer, follows = behind(j)
+
+        @pl.when(follows)
+        def _(j=j, peer=peer):
+            pl.semaphore_signal(answer.at[j - 1], inc=1, device_id=peer, device_id_type=MESH)
+
+    for b, (bit, other) in enumerate(row_pairs):
+        @pl.when(bit == 1)
+        def _(b=b, other=other):
+            pl.semaphore_signal(answer.at[N - 1 + b], inc=1, device_id=(other, d), device_id_type=MESH)
 
     first_rows = n * entry // units
 
@@ -88,12 +120,21 @@
                 device_id=(r, t),
                 device_id_type=MESH,
             )
-            for k, t in enumerate(dim_peers)
+            for k, t in enumerate(dim_peers if piece else [lax.rem(d + j, N) for j in range(1, N)])
         ]
 
     a2a = [slab_copies(0), slab_copies(1)]
-    for copy in a2a[0]:
-        copy.start()
+
+    for j in range(1, N):
+        @pl.when(d >= j)
+        def _(j=j):
+            a2a[0][N - j - 1].start()
+
+    for j in range(1, N):
+        @pl.when(d + j < N)
+        def _(j=j):
+            pl.semaphore_wait(answer.at[j - 1], 1)
+            a2a[0][j - 1].start()
 
     @pl.when(core == 0)
     def _():
@@ -136,6 +177,11 @@
             return carry
 
         lax.fori_loop(0, h // rows, add, 0)
+
+    for b, (bit, other) in enumerate(row_pairs):
+        @pl.when(bit == 0)
+        def _(b=b):
+            pl.semaphore_wait(answer.at[N - 1 + b], 1)
 
     row_bits = list(range(nrow))
     orders = [row_bits, row_bits[:1] + row_bits[:0:-1]]
@@ -370,6 +416,21 @@
     for copies in a2a:
         for copy in copies:
             copy.wait()
+
+
+def place(parts, serving, share, serving_out, share_out, sems):
+    rows = serving.shape[0] // parts
+    copies = [
+        pltpu.make_async_copy(
+            serving.at[pl.ds(i * rows, rows), :], serving_out.at[pl.ds(i * rows, rows), :], sems.at[i]
+        )
+        for i in range(parts)
+    ]
+    copies.append(pltpu.make_async_copy(share, share_out, sems.at[parts]))
+    for copy in copies:
+        copy.start()
+    for copy in copies:
+        copy.wait()
 
 
 def shards(entity_table, relations, thresholds, head_ids, rel_ids, thr_idx):
@@ -428,11 +489,24 @@
             DMA((bits_of(R),)), DMA((bits_of(R),)),
             DMA((N - 1,)), DMA((N - 1,)),
             DMA((1,)), DMA((1,)),
+            pltpu.SemaphoreType.REGULAR((N - 1 + bits_of(R),)),
         ],
         compiler_params=pltpu.CompilerParams(
             collective_id=0, has_side_effects=True, vmem_limit_bytes=40 * 2**20
         ),
     )(*[pltpu.with_memory_space_constraint(x, pltpu.HBM) for x in operands])
+    parts = 8
+    serving, share = pl.pallas_call(
+        functools.partial(place, parts),
+        out_shape=(
+            jax.ShapeDtypeStruct(serving.shape, f32),
+            jax.ShapeDtypeStruct(share.shape, f32),
+        ),
+        in_specs=[vmem] * 2,
+        out_specs=(anywhere, anywhere),
+        scratch_shapes=[DMA((parts + 1,))],
+        compiler_params=pltpu.CompilerParams(vmem_limit_bytes=4 * 2**20),
+    )(*[pltpu.with_memory_space_constraint(x, pltpu.VMEM) for x in (serving, share)])
     return serving, share.reshape(mine)
 
 

time: 200 us -> 199 us (level)
  local copies, waits for them, and re-layouts: 3.91 us -> 0 us
  Pallas kernels: 196 us -> 198 us
    unnamed x2 -> x0, local copies, waits for them, and re-layouts: 3.91 us -> none
    pallas_call x0 -> x1, Pallas kernels: none -> 3.38 us  [shards(): pl.pallas_call(functools.partial(place, parts), out_shape=(jax.ShapeDtype...]
where the time goes in v3:
time: 199 us
  Pallas kernels  198 us (99%)
    pallas_call x1, Pallas kernels, shards(): pl.pallas_call(functools.partial(kernel, R, N, n * R * N), out_shape=(plt...  195 us

profile of v3, /device:TPU:9, one launch (start us, length us, event | category | flops | bytes accessed | tf_op | source)
XLA Modules:
  0.0 199.1 jit_solution(1131190131344098560)
XLA Ops:
  0.6 195.0 %shard_map.77 = (f32[16384,128]{1,0:T(8,128)S(1)}, f32[1,64]{1,0:T(1,128)S(1)}) custom-call(s32[2048]{0:T(1024)} %head_ids_.1, s32[2048]{0:T(1024)} %rel_ids_.1, f32[64]{0:T(128)} %thr_.1, s32[16,1,128]{2,1,0:T(1,128)} %bitcast.2, f32[822,512]{1,0:T(8,128)} %rel_.1, f32[4096,512]{1,0:T(8,128)} %table.1), custom_call_target="tpu_custom_call" | custom-call | tf_op jit(solution)/shard_map/pallas_call | solution.py:453
  195.7 3.4 %shard_map.78 = (f32[16384,128]{1,0:T(8,128)}, f32[1,64]{1,0:T(1,128)}) custom-call(f32[16384,128]{1,0:T(8,128)S(1)} %get-tuple-element.6.serving, f32[1,64]{1,0:T(1,128)S(1)} %get-tuple-element.7.share), custom_call_target="tpu_custom_call" | custom-call | tf_op jit(solution)/shard_map/pallas_call | solution.py:499

commit v4 on v3

--- a/solution.py
+++ b/solution.py
@@ -78,18 +78,6 @@
         def _(other=other):
             pl.semaphore_signal(barrier, inc=1, device_id=(other, d), device_id_type=MESH)
 
-    load = pltpu.make_async_copy(table, tab, load_sem)
-    load.start()
-    own = pltpu.make_async_copy(
-        slab_rows(d, 0, n),
-        serving.at[pl.ds(pl.multiple_of(d * n, 8), n), :],
-        own_sem,
-    )
-    own.start()
-    pairs = [(head_ids_, head_ids), (rel_ids_, rel_ids), (thr_, thr), (thr_idx_, thr_idx), (rel_, rel)]
-    args = [pltpu.make_async_copy(src, dst, arg_sem.at[i]) for i, (src, dst) in enumerate(pairs)]
-    for copy in args:
-        copy.start()
 
     @pl.when(leaders > 0)
     def _():
@@ -129,6 +117,19 @@
         @pl.when(d >= j)
         def _(j=j):
             a2a[0][N - j - 1].start()
+
+    load = pltpu.make_async_copy(table, tab, load_sem)
+    load.start()
+    own = pltpu.make_async_copy(
+        slab_rows(d, 0, n),
+        serving.at[pl.ds(pl.multiple_of(d * n, 8), n), :],
+        own_sem,
+    )
+    own.start()
+    pairs = [(head_ids_, head_ids), (rel_ids_, rel_ids), (thr_, thr), (thr_idx_, thr_idx), (rel_, rel)]
+    args = [pltpu.make_async_copy(src, dst, arg_sem.at[i]) for i, (src, dst) in enumerate(pairs)]
+    for copy in args:
+        copy.start()
 
     for j in range(1, N):
         @pl.when(d + j < N)
@@ -211,7 +212,7 @@
                 return carry
 
             lax.fori_loop(0, n // 128, narrow, 0)
-        if k == 1:
+        if k == min(1, nrow - 1):
             idx = thr_idx[...]
 
             def choose(t, acc):

time: 199 us -> 199 us (level)
  no operation moved by 1% of the time
where the time goes in v4:
time: 199 us
  Pallas kernels  198 us (99%)
    pallas_call x1, Pallas kernels, shards(): pl.pallas_call(functools.partial(kernel, R, N, n * R * N), out_shape=(plt...  195 us

profile of v4, /device:TPU:9, one launch (start us, length us, event | category | flops | bytes accessed | tf_op | source)
XLA Modules:
  0.0 199.1 jit_solution(2668322044461423617)
XLA Ops:
  0.6 195.0 %shard_map.77 = (f32[16384,128]{1,0:T(8,128)S(1)}, f32[1,64]{1,0:T(1,128)S(1)}) custom-call(s32[2048]{0:T(1024)} %head_ids_.1, s32[2048]{0:T(1024)} %rel_ids_.1, f32[64]{0:T(128)} %thr_.1, s32[16,1,128]{2,1,0:T(1,128)} %bitcast.2, f32[822,512]{1,0:T(8,128)} %rel_.1, f32[4096,512]{1,0:T(8,128)} %table.1), custom_call_target="tpu_custom_call" | custom-call | tf_op jit(solution)/shard_map/pallas_call | solution.py:454
  195.7 3.4 %shard_map.78 = (f32[16384,128]{1,0:T(8,128)}, f32[1,64]{1,0:T(1,128)}) custom-call(f32[16384,128]{1,0:T(8,128)S(1)} %get-tuple-element.6.serving, f32[1,64]{1,0:T(1,128)S(1)} %get-tuple-element.7.share), custom_call_target="tpu_custom_call" | custom-call | tf_op jit(solution)/shard_map/pallas_call | solution.py:500

commit v5 on v4

--- a/solution.py
+++ b/solution.py
@@ -21,14 +21,14 @@
 def kernel(
     R, N, total_ents, head_ids_, rel_ids_, thr_, thr_idx_, rel_, table, *others
 ):
-    slabs = others[:-41]
+    slabs = others[:-42]
     (
         serving, frac_out,
         head_ids, rel_ids, thr, thr_idx, rel, arg_sem,
         tab, low, part, recv, full, zsum, zin, zout, qb, lev, frac, fr_pair, fr_in, fr_dim, fr_sum, fr_all,
         load_sem, own_sem, a2a_send, a2a_recv, ex_send, ex_recv, z_send, z_recv,
-        pair_send, pair_recv, f_send, f_recv, g_send, g_recv, last_send, last_recv, answer,
-    ) = others[-41:]
+        pair_send, pair_recv, f_send, f_recv, g_send, g_recv, last_send, last_recv, answer, word,
+    ) = others[-42:]
     r = lax.axis_index("rows")
     d = lax.axis_index("dim")
     core = lax.rem(r, 2)
@@ -71,10 +71,11 @@
         def _(peer=peer):
             pl.semaphore_signal(barrier, inc=1, device_id=peer, device_id_type=MESH)
 
+    at_head = d == 0
     for bit, other in row_pairs:
-        leaders = leaders + bit
-
-        @pl.when(bit == 0)
+        leaders = leaders + jnp.where(at_head, bit, 0)
+
+        @pl.when(jnp.logical_and(at_head, bit == 0))
         def _(other=other):
             pl.semaphore_signal(barrier, inc=1, device_id=(other, d), device_id_type=MESH)
 
@@ -91,7 +92,7 @@
             pl.semaphore_signal(answer.at[j - 1], inc=1, device_id=peer, device_id_type=MESH)
 
     for b, (bit, other) in enumerate(row_pairs):
-        @pl.when(bit == 1)
+        @pl.when(jnp.logical_and(at_head, bit == 1))
         def _(b=b, other=other):
             pl.semaphore_signal(answer.at[N - 1 + b], inc=1, device_id=(other, d), device_id_type=MESH)
 
@@ -142,6 +143,19 @@
         for copy in a2a[1]:
             copy.start()
 
+    @pl.when(at_head)
+    def _():
+        for b, (bit, other) in enumerate(row_pairs):
+            @pl.when(bit == 0)
+            def _(b=b):
+                pl.semaphore_wait(answer.at[N - 1 + b], 1)
+
+            pl.semaphore_signal(word.at[b], inc=1, device_id=(other, d), device_id_type=MESH)
+        for b in range(nrow):
+            pl.semaphore_wait(word.at[b], 1)
+            for j in range(1, N):
+                pl.semaphore_signal(word.at[b], inc=1, device_id=(r, lax.rem(d + j, N)), device_id_type=MESH)
+
     for copy in args:
         copy.wait()
     load.wait()
@@ -179,10 +193,10 @@
 
         lax.fori_loop(0, h // rows, add, 0)
 
-    for b, (bit, other) in enumerate(row_pairs):
-        @pl.when(bit == 0)
-        def _(b=b):
-            pl.semaphore_wait(answer.at[N - 1 + b], 1)
+    @pl.when(d > 0)
+    def _():
+        for b in range(nrow):
+            pl.semaphore_wait(word.at[b], 1)
 
     row_bits = list(range(nrow))
     orders = [row_bits, row_bits[:1] + row_bits[:0:-1]]
@@ -491,6 +505,7 @@
             DMA((N - 1,)), DMA((N - 1,)),
             DMA((1,)), DMA((1,)),
             pltpu.SemaphoreType.REGULAR((N - 1 + bits_of(R),)),
+            pltpu.SemaphoreType.REGULAR((bits_of(R),)),
         ],
         compiler_params=pltpu.CompilerParams(
             collective_id=0, has_side_effects=True, vmem_limit_bytes=40 * 2**20

time: 199 us -> 199 us (level)
  no operation moved by 1% of the time
where the time goes in v5:
time: 199 us
  Pallas kernels  198 us (99%)
    pallas_call x1, Pallas kernels, shards(): pl.pallas_call(functools.partial(kernel, R, N, n * R * N), out_shape=(plt...  195 us

profile of v5, /device:TPU:9, one launch (start us, length us, event | category | flops | bytes accessed | tf_op | source)
XLA Modules:
  0.0 198.6 jit_solution(14325549550386863662)
XLA Ops:
  0.6 194.5 %shard_map.77 = (f32[16384,128]{1,0:T(8,128)S(1)}, f32[1,64]{1,0:T(1,128)S(1)}) custom-call(s32[2048]{0:T(1024)} %head_ids_.1, s32[2048]{0:T(1024)} %rel_ids_.1, f32[64]{0:T(128)} %thr_.1, s32[16,1,128]{2,1,0:T(1,128)} %bitcast.2, f32[822,512]{1,0:T(8,128)} %rel_.1, f32[4096,512]{1,0:T(8,128)} %table.1), custom_call_target="tpu_custom_call" | custom-call | tf_op jit(solution)/shard_map/pallas_call | solution.py:468
  195.2 3.4 %shard_map.78 = (f32[16384,128]{1,0:T(8,128)}, f32[1,64]{1,0:T(1,128)}) custom-call(f32[16384,128]{1,0:T(8,128)S(1)} %get-tuple-element.6.serving, f32[1,64]{1,0:T(1,128)S(1)} %get-tuple-element.7.share), custom_call_target="tpu_custom_call" | custom-call | tf_op jit(solution)/shard_map/pallas_call | solution.py:515

commit v6 on v5

--- a/solution.py
+++ b/solution.py
@@ -91,10 +91,6 @@
         def _(j=j, peer=peer):
             pl.semaphore_signal(answer.at[j - 1], inc=1, device_id=peer, device_id_type=MESH)
 
-    for b, (bit, other) in enumerate(row_pairs):
-        @pl.when(jnp.logical_and(at_head, bit == 1))
-        def _(b=b, other=other):
-            pl.semaphore_signal(answer.at[N - 1 + b], inc=1, device_id=(other, d), device_id_type=MESH)
 
     first_rows = n * entry // units
 
@@ -118,6 +114,11 @@
         @pl.when(d >= j)
         def _(j=j):
             a2a[0][N - j - 1].start()
+
+    for b, (bit, other) in enumerate(row_pairs):
+        @pl.when(jnp.logical_and(at_head, bit == 1))
+        def _(b=b, other=other):
+            pl.semaphore_signal(answer.at[N - 1 + b], inc=1, device_id=(other, d), device_id_type=MESH)
 
     load = pltpu.make_async_copy(table, tab, load_sem)
     load.start()
@@ -441,7 +442,7 @@
         )
         for i in range(parts)
     ]
-    copies.append(pltpu.make_async_copy(share, share_out, sems.at[parts]))
+    copies.insert(0, pltpu.make_async_copy(share, share_out, sems.at[parts]))
     for copy in copies:
         copy.start()
     for copy in copies:

time: 199 us -> 199 us (level)
  no operation moved by 1% of the time
where the time goes in v6:
time: 199 us
  Pallas kernels  198 us (99%)
    pallas_call x1, Pallas kernels, shards(): pl.pallas_call(functools.partial(kernel, R, N, n * R * N), out_shape=(plt...  195 us

profile of v6, /device:TPU:9, one launch (start us, length us, event | category | flops | bytes accessed | tf_op | source)
XLA Modules:
  0.0 198.6 jit_solution(14527943725590018093)
XLA Ops:
  0.6 194.5 %shard_map.77 = (f32[16384,128]{1,0:T(8,128)S(1)}, f32[1,64]{1,0:T(1,128)S(1)}) custom-call(s32[2048]{0:T(1024)} %head_ids_.1, s32[2048]{0:T(1024)} %rel_ids_.1, f32[64]{0:T(128)} %thr_.1, s32[16,1,128]{2,1,0:T(1,128)} %bitcast.2, f32[822,512]{1,0:T(8,128)} %rel_.1, f32[4096,512]{1,0:T(8,128)} %table.1), custom_call_target="tpu_custom_call" | custom-call | tf_op jit(solution)/shard_map/pallas_call | solution.py:469
  195.2 3.4 %shard_map.78 = (f32[16384,128]{1,0:T(8,128)}, f32[1,64]{1,0:T(1,128)}) custom-call(f32[16384,128]{1,0:T(8,128)S(1)} %get-tuple-element.6.serving, f32[1,64]{1,0:T(1,128)S(1)} %get-tuple-element.7.share), custom_call_target="tpu_custom_call" | custom-call | tf_op jit(solution)/shard_map/pallas_call | solution.py:516
